TPU v7x, 256 devices: a whole 4x4x8 slice. The times are simulated.
256 devices in a mesh: rep: 32 (over z_lo, x, core), ep: 8 (over z_hi, y).
Axes of the slice: x: 4, y: 4, z: 8 (z_hi: 2, z_lo: 4; z = z_hi * 4 + z_lo), core: 2. Of those that a mesh axis runs over, the one named last changes fastest.
Arguments:
- tokens: bfloat16 [2, 1024, 4096], P(None, 'ep', 'rep'), may hold values from -6 to 6
- expert_ids: int32 [2, 1024, 2], P(None, 'ep'), may hold values from 0 to 7, all different within a row; in each aligned block of 128 rows (0 to 127, 128 to 255, ..., all dimensions but the last counted through in order) at most 48 rows name the same one
- router_weight: bfloat16 [4096, 8], P('rep'), may hold values from -0.09375 to 0.09375
- w_gate: bfloat16 [8, 4096, 8192], P('ep', None, 'rep'), may hold values from -0.09375 to 0.09375
- w_up: bfloat16 [8, 4096, 8192], P('ep', None, 'rep'), may hold values from -0.09375 to 0.09375
- w_down: bfloat16 [8, 8192, 4096], P('ep', 'rep'), may hold values from -0.0625 to 0.0625
- cotangent: bfloat16 [2, 1024, 4096], P(None, 'ep', 'rep'), may hold values from -6 to 6
Outputs:
- mixed: bfloat16 [2, 1024, 4096], P(None, 'ep', 'rep')
- token_grad: bfloat16 [2, 1024, 4096], P(None, 'ep', 'rep')
- gate_grad: bfloat16 [8, 4096, 8192], P('ep', None, 'rep')
- up_grad: bfloat16 [8, 4096, 8192], P('ep', None, 'rep')
- down_grad: bfloat16 [8, 8192, 4096], P('ep', 'rep')
- router_grad: float32 [4096, 8], P('rep')
Inputs may be any that keep to these rules, and one draw needn't show every extreme that they name: `expert_ids`: each row names 2 different experts. Among the 128 rows of one index of ep in one microbatch no expert is named by more than 48 rows, and in every draw some expert is named by exactly 48 of them.
All inputs are finite; a program needn't handle non-finite values.
Results may differ from a plain program's by a relative error of at most 0.025.
Values may be sent and summed in bfloat16 or wider, within the bound.
A program may use at most 128 MiB of HBM per device.

v0:
```python
import jax
import jax.numpy as jnp
from jax import lax
from jax.sharding import Mesh
from jax.sharding import PartitionSpec as P

TOP = 2
REP = ("rep_0", "rep_1", "rep_2")


def copy_for_each(array, axis):
    devices = lax.axis_size(axis)
    return lax.all_to_all(
        jnp.broadcast_to(array[None], (devices, *array.shape)), axis, 0, 0, tiled=True
    )


def taken_together(array, axis):
    everything = copy_for_each(array, axis)
    return jnp.sum(everything, axis=0)


def split_up(array, dim, devices):
    dims = array.shape
    blocks = array.reshape(*dims[:dim], devices, dims[dim] // devices, *dims[dim + 1 :])
    return jnp.moveaxis(blocks, dim, 0)


def summed_on_arrival(array, axis, dim):
    blocks = split_up(array, dim, lax.axis_size(axis))
    arrived = lax.all_to_all(blocks, axis, split_axis=0, concat_axis=0, tiled=True)
    return arrived.astype(jnp.float32).sum(axis=0)


def sum_by_axis(array, axes, dim):
    far, near = axes
    blocks = split_up(array, dim, lax.axis_size(far))
    nearer = summed_on_arrival(blocks, near, dim + 1)
    arrived = lax.all_to_all(
        nearer.astype(jnp.bfloat16), far, split_axis=0, concat_axis=0, tiled=True
    )
    return arrived.astype(jnp.float32).sum(axis=0)


def contract_first(left, right):
    return lax.dot_general(
        left, right, (((0,), (0,)), ((), ())), preferred_element_type=jnp.float32
    )


def contract_last(left, right):
    return lax.dot_general(
        left, right, (((1,), (1,)), ((), ())), preferred_element_type=jnp.float32
    )


def route(route_ids, experts, capacity, slot_count):
    hits = route_ids[:, :, None] == jnp.arange(experts, dtype=jnp.int32)[None, None, :]
    per_token = jnp.sum(hits.astype(jnp.int32), axis=1)
    before = jnp.cumsum(per_token, axis=0) - per_token
    places = jnp.sum(jnp.where(hits, before[:, None, :], 0), axis=2)
    slots = route_ids * capacity + places
    match = jnp.arange(slot_count, dtype=jnp.int32)[:, None, None] == slots[None, :, :]
    token_count = route_ids.shape[0]
    source_row = jnp.sum(
        jnp.where(match, jnp.arange(token_count, dtype=jnp.int32)[None, :, None], 0), axis=(1, 2)
    )
    filled = jnp.any(match, axis=(1, 2))
    return (hits, slots, match, source_row, filled)


def pack(rows, source_row, filled, scale):
    picked = jnp.take(rows, source_row, axis=0)
    if scale is None:
        return jnp.where(filled[:, None], picked, jnp.zeros_like(picked))
    return (picked.astype(jnp.float32) * scale[:, None]).astype(jnp.bfloat16)


def deliver(rows, source_row, filled, scale):
    moved = lax.all_to_all(
        pack(rows, source_row, filled, scale), "ep", split_axis=0, concat_axis=0, tiled=True
    )
    result = lax.all_gather(moved, REP, axis=1, tiled=True)
    return result


def collect(columns):
    return lax.all_to_all(columns, "ep", split_axis=1, concat_axis=1, tiled=True)


def shards(tokens, expert_ids, router_weight, w_gate, w_up, w_down, cotangent):
    micro_count = tokens.shape[0]
    tok_rows = tokens.shape[1]
    experts = router_weight.shape[1]
    capacity = min(tok_rows, 3 * tok_rows * TOP // (2 * experts))
    slot_count = lax.axis_size("ep") * capacity
    gate_w = w_gate[0]
    up_w = w_up[0]
    down_w = w_down[0]
    gate_acc = jnp.zeros(gate_w.shape, jnp.float32)
    up_acc = jnp.zeros(up_w.shape, jnp.float32)
    down_acc = jnp.zeros(down_w.shape, jnp.float32)
    router_acc = jnp.zeros(router_weight.shape, jnp.float32)
    router_wide = router_weight.astype(jnp.float32)
    all_logits = taken_together(
        jnp.einsum("mtc,ce->mte", tokens, router_weight, preferred_element_type=jnp.float32), REP
    )
    mixed = []
    token_grad = []
    for step in range(micro_count):
        route_ids = expert_ids[step]
        hits, slots, match, source_row, filled = route(route_ids, experts, capacity, slot_count)
        logits = all_logits[step]
        chosen = jnp.sum(jnp.where(hits, logits[:, None, :], 0.0), axis=2)
        spread = chosen[:, 0] - chosen[:, 1]
        first = jax.nn.sigmoid(spread)
        second = jax.nn.sigmoid(-spread)
        gates = jnp.stack([first, second], axis=1)
        slot_gate = jnp.sum(jnp.where(match, gates[None, :, :], 0.0), axis=(1, 2))
        expert_rows = deliver(tokens[step], source_row, filled, None)
        pre_gate = jnp.dot(expert_rows, gate_w, preferred_element_type=jnp.float32)
        pre_up = jnp.dot(expert_rows, up_w, preferred_element_type=jnp.float32)
        gate_sig = jax.nn.sigmoid(pre_gate)
        gate_act = pre_gate * gate_sig
        hidden = (gate_act * pre_up).astype(jnp.bfloat16)
        outputs = sum_by_axis(
            lax.dot_general(
                down_w, hidden, (((0,), (1,)), ((), ())), preferred_element_type=jnp.float32
            ).astype(jnp.bfloat16),
            (("rep_0", "rep_1"), "rep_2"),
            0,
        ).astype(jnp.bfloat16)
        returned = collect(outputs)
        first_out = jnp.take(returned, slots[:, 0], axis=1).astype(jnp.float32)
        second_out = jnp.take(returned, slots[:, 1], axis=1).astype(jnp.float32)
        mixed.append(
            (first[None, :] * first_out + second[None, :] * second_out).T.astype(jnp.bfloat16)
        )
        cot_cols = cotangent[step].T.astype(jnp.float32)
        partial_dots = jnp.stack(
            [jnp.sum(cot_cols * first_out, axis=0), jnp.sum(cot_cols * second_out, axis=0)]
        )
        gate_dots = taken_together(partial_dots, REP)
        delta = (gate_dots[0] - gate_dots[1]) * first * second
        logit_grad = delta[:, None] * (
            hits[:, 0].astype(jnp.float32) - hits[:, 1].astype(jnp.float32)
        )
        router_acc = router_acc + jnp.dot(
            tokens[step].astype(jnp.float32).T, logit_grad, precision=lax.Precision.HIGHEST
        )
        router_in = jnp.dot(logit_grad, router_wide.T, precision=lax.Precision.HIGHEST)
        expert_cots = deliver(cotangent[step], source_row, filled, slot_gate)
        hidden_grad = contract_last(expert_cots, down_w)
        gate_pre_grad = (
            hidden_grad * pre_up * (gate_sig * (1.0 + pre_gate * (1.0 - gate_sig)))
        ).astype(jnp.bfloat16)
        up_pre_grad = (hidden_grad * gate_act).astype(jnp.bfloat16)
        down_acc = down_acc + contract_first(hidden, expert_cots)
        gate_acc = gate_acc + contract_first(expert_rows, gate_pre_grad)
        up_acc = up_acc + contract_first(expert_rows, up_pre_grad)
        input_cols = sum_by_axis(
            (contract_last(gate_w, gate_pre_grad) + contract_last(up_w, up_pre_grad)).astype(
                jnp.bfloat16
            ),
            (("rep_0", "rep_1"), "rep_2"),
            0,
        ).astype(jnp.bfloat16)
        returned_grad = collect(input_cols)
        grad_cols = jnp.take(returned_grad, slots[:, 0], axis=1).astype(jnp.float32)
        grad_cols = grad_cols + jnp.take(returned_grad, slots[:, 1], axis=1).astype(jnp.float32)
        token_grad.append((grad_cols + router_in.T).T.astype(jnp.bfloat16))
    router_total = taken_together(router_acc, "ep")
    return (
        jnp.stack(mixed),
        jnp.stack(token_grad),
        gate_acc.astype(jnp.bfloat16)[None],
        up_acc.astype(jnp.bfloat16)[None],
        down_acc.astype(jnp.bfloat16)[None],
        router_total,
    )


def solution(mesh):
    split = Mesh(mesh.devices.reshape(4, 4, 2, mesh.shape["ep"]), ("rep_0", "rep_1", "rep_2", "ep"))
    in_specs = (
        P(None, "ep", REP),
        P(None, "ep", None),
        P(REP, None),
        P("ep", None, REP),
        P("ep", None, REP),
        P("ep", REP, None),
        P(None, "ep", REP),
    )
    out_specs = (
        P(None, "ep", REP),
        P(None, "ep", REP),
        P("ep", None, REP),
        P("ep", None, REP),
        P("ep", REP, None),
        P(REP, None),
    )
    return jax.shard_map(
        shards, mesh=split, in_specs=in_specs, out_specs=out_specs, check_vma=False
    )
```

profile of v0, /device:TPU:32, one launch (start us, length us, event | category | flops | bytes accessed | tf_op | source)
XLA Modules:
  0.0 662.5 jit_solution(15481597892796571032)
XLA Ops:
  12.3 20.5 %all_to_all.156 = bf16[8,48,128]{2,1,0:T(8,128)(2,1)} all-to-all(bf16[8,48,128]{2,1,0:T(8,128)(2,1)S(1)} %bitcast.283), channel_id=1, replica_groups=mesh['rep_0'=4,'rep_1'=4,'rep_2'=2,'ep'=8] {'ep'}, dimensions={0} | all-to-all | bytes 196608 | tf_op jit(solution)/shard_map/all_to_all | solution.py:80
  34.8 13.4 %all_to_all.157 = bf16[8,48,128]{2,1,0:T(8,128)(2,1)} all-to-all(bf16[8,48,128]{2,1,0:T(8,128)(2,1)S(1)} %bitcast.284), channel_id=1, replica_groups=mesh['rep_0'=4,'rep_1'=4,'rep_2'=2,'ep'=8] {'ep'}, dimensions={0} | all-to-all | bytes 196608 | tf_op jit(solution)/shard_map/all_to_all | solution.py:80
  48.4 47.2 %all-gather.5.cloned.1.call-done = bf16[384,4096]{1,0:T(8,128)(2,1)} async-done(((bf16[384,128]{1,0:T(8,128)(2,1)}), bf16[384,4096]{1,0:T(8,128)(2,1)}) %all-gather.5.cloned.1.call-update) | async-done | bytes 3145744 | tf_op jit(solution)/shard_map/all_gather | solution.py:83
  104.2 6.1 reshape_reshape.12
  119.5 43.7 %all-gather.7.cloned.1.call-done = bf16[384,4096]{1,0:T(8,128)(2,1)} async-done(((bf16[384,128]{1,0:T(8,128)(2,1)}), bf16[384,4096]{1,0:T(8,128)(2,1)}) %all-gather.7.cloned.1.call-update) | async-done | bytes 3145744 | tf_op jit(solution)/shard_map/all_gather | solution.py:83
  168.2 5.6 all-to-all-start
  187.9 6.1 reshape_reshape.13
  198.0 10.4 %all_to_all.158 = bf16[2,16,128,384]{2,1,3,0:T(8,128)(2,1)} all-to-all(bf16[2,16,128,384]{2,1,3,0:T(8,128)(2,1)} %bitcast.267), channel_id=1, replica_groups=mesh['rep_0'=4,'rep_1'=4,'rep_2'=2,'ep'=8] {'rep_2'}, dimensions={0} | all-to-all | bytes 6291456 | tf_op jit(solution)/shard_map/all_to_all | solution.py:31
  208.3 8.0 %all-to-all-start.3 = ((bf16[16,128,384]{1,2,0:T(8,128)(2,1)}), bf16[16,128,384]{1,2,0:T(8,128)(2,1)}, u32[]{:S(2)}, u32[]{:S(2)}) async-start(bf16[16,128,384]{1,2,0:T(8,128)(2,1)} %copy.78), calls=%async_computation.3 | async-start | bytes 3145728 | tf_op jit(solution)/shard_map/all_to_all | solution.py:39
  223.4 30.0 %all-to-all-done.3 = bf16[16,128,384]{1,2,0:T(8,128)(2,1)} async-done(((bf16[16,128,384]{1,2,0:T(8,128)(2,1)}), bf16[16,128,384]{1,2,0:T(8,128)(2,1)}, u32[]{:S(2)}, u32[]{:S(2)}) %all-to-all-start.3) | async-done | bytes 1572896 | tf_op jit(solution)/shard_map/all_to_all | solution.py:39
  253.4 5.5 all-to-all-start.7
  262.8 32.1 %all-to-all-done.7 = bf16[16,128,384]{1,2,0:T(8,128)(2,1)} async-done(((bf16[16,128,384]{1,2,0:T(8,128)(2,1)}), bf16[16,128,384]{1,2,0:T(8,128)(2,1)}, u32[]{:S(2)}, u32[]{:S(2)}) %all-to-all-start.7) | async-done | bytes 1572896 | tf_op jit(solution)/shard_map/all_to_all | solution.py:39
  294.8 7.8 %all-to-all-start.4 = ((bf16[128,8,48]{0,2,1:T(8,128)(2,1)}), bf16[128,8,48]{0,2,1:T(8,128)(2,1)S(1)}, u32[]{:S(2)}, u32[]{:S(2)}) async-start(bf16[128,8,48]{0,2,1:T(8,128)(2,1)} %bitcast.15), calls=%async_computation.4 | async-start | bytes 196608 | tf_op jit(solution)/shard_map/all_to_all | solution.py:88
  305.0 8.2 %all-to-all-done.4 = bf16[128,8,48]{0,2,1:T(8,128)(2,1)S(1)} async-done(((bf16[128,8,48]{0,2,1:T(8,128)(2,1)}), bf16[128,8,48]{0,2,1:T(8,128)(2,1)S(1)}, u32[]{:S(2)}, u32[]{:S(2)}) %all-to-all-start.4) | async-done | bytes 98336 | tf_op jit(solution)/shard_map/all_to_all | solution.py:88
  318.0 8.9 %all-to-all-done.8 = bf16[128,8,48]{0,2,1:T(8,128)(2,1)S(1)} async-done(((bf16[128,8,48]{0,2,1:T(8,128)(2,1)}), bf16[128,8,48]{0,2,1:T(8,128)(2,1)S(1)}, u32[]{:S(2)}, u32[]{:S(2)}) %all-to-all-start.8) | async-done | bytes 98336 | tf_op jit(solution)/shard_map/all_to_all | solution.py:88
  329.1 6.1 all-to-all-start.18
  335.3 6.5 all-to-all-done.18
  342.2 14.1 %all_to_all.159 = bf16[8,48,128]{2,1,0:T(8,128)(2,1)} all-to-all(bf16[8,48,128]{2,1,0:T(8,128)(2,1)S(1)} %bitcast.281), channel_id=1, replica_groups=mesh['rep_0'=4,'rep_1'=4,'rep_2'=2,'ep'=8] {'ep'}, dimensions={0} | all-to-all | bytes 196608 | tf_op jit(solution)/shard_map/all_to_all | solution.py:80
  362.8 6.6 all-to-all-done.13
  369.8 14.3 %all_to_all.160 = bf16[8,48,128]{2,1,0:T(8,128)(2,1)} all-to-all(bf16[8,48,128]{2,1,0:T(8,128)(2,1)S(1)} %bitcast.282), channel_id=1, replica_groups=mesh['rep_0'=4,'rep_1'=4,'rep_2'=2,'ep'=8] {'ep'}, dimensions={0} | all-to-all | bytes 196608 | tf_op jit(solution)/shard_map/all_to_all | solution.py:80
  384.5 33.7 %all-gather.11.cloned.1.call-done = bf16[384,4096]{1,0:T(8,128)(2,1)} async-done(((bf16[384,128]{1,0:T(8,128)(2,1)}), bf16[384,4096]{1,0:T(8,128)(2,1)}) %all-gather.11.cloned.1.call-update) | async-done | bytes 3145744 | tf_op jit(solution)/shard_map/all_gather | solution.py:83
  425.8 6.1 reshape_reshape.15
  441.2 44.8 %all-gather.9.cloned.1.call-done = bf16[384,4096]{1,0:T(8,128)(2,1)} async-done(((bf16[384,128]{1,0:T(8,128)(2,1)}), bf16[384,4096]{1,0:T(8,128)(2,1)}) %all-gather.9.cloned.1.call-update) | async-done | bytes 3145744 | tf_op jit(solution)/shard_map/all_gather | solution.py:83
  493.6 8.1 %all-to-all-start.19 = ((f32[8,128,8]{1,2,0:T(8,128)}), f32[8,128,8]{1,2,0:T(8,128)S(1)}, u32[]{:S(2)}, u32[]{:S(2)}) async-start(f32[8,128,8]{1,2,0:T(8,128)} %broadcast_in_dim.184), calls=%async_computation.19 | async-start | bytes 65536 | tf_op jit(solution)/shard_map/all_to_all | solution.py:13
  501.6 5.5 fusion.5
  512.2 6.1 reshape_reshape.14
  522.2 10.3 %all_to_all.161 = bf16[2,16,128,384]{2,1,3,0:T(8,128)(2,1)} all-to-all(bf16[2,16,128,384]{2,1,3,0:T(8,128)(2,1)} %bitcast.268), channel_id=1, replica_groups=mesh['rep_0'=4,'rep_1'=4,'rep_2'=2,'ep'=8] {'rep_2'}, dimensions={0} | all-to-all | bytes 6291456 | tf_op jit(solution)/shard_map/all_to_all | solution.py:31
  544.9 29.9 %all-to-all-done.16 = bf16[16,128,384]{1,2,0:T(8,128)(2,1)S(1)} async-done(((bf16[16,128,384]{1,2,0:T(8,128)(2,1)}), bf16[16,128,384]{1,2,0:T(8,128)(2,1)S(1)}, u32[]{:S(2)}, u32[]{:S(2)}) %all-to-all-start.16) | async-done | bytes 1572896 | tf_op jit(solution)/shard_map/all_to_all | solution.py:39
  575.9 5.8 all-to-all-start.11
  596.0 21.4 %all-to-all-done.11 = bf16[16,128,384]{1,2,0:T(8,128)(2,1)S(1)} async-done(((bf16[16,128,384]{1,2,0:T(8,128)(2,1)}), bf16[16,128,384]{1,2,0:T(8,128)(2,1)S(1)}, u32[]{:S(2)}, u32[]{:S(2)}) %all-to-all-start.11) | async-done | bytes 1572896 | tf_op jit(solution)/shard_map/all_to_all | solution.py:39
  617.4 9.6 %all-to-all-start.17 = ((bf16[128,8,48]{0,2,1:T(8,128)(2,1)}), bf16[128,8,48]{0,2,1:T(8,128)(2,1)S(1)}, u32[]{:S(2)}, u32[]{:S(2)}) async-start(bf16[128,8,48]{0,2,1:T(8,128)(2,1)} %bitcast.65), calls=%async_computation.17 | async-start | bytes 196608 | tf_op jit(solution)/shard_map/all_to_all | solution.py:88
  642.6 5.9 fusion.7
  (162 shorter events, 159.8 us)
Async XLA Ops:
  7.2 94.3 %copy-start = (bf16[1,256,4096]{2,1,0:T(8,128)(2,1)S(1)}, bf16[1,256,4096]{2,1,0:T(8,128)(2,1)}, u32[]{:S(2)}) copy-start(bf16[1,256,4096]{2,1,0:T(8,128)(2,1)} %param.16) | copy-start | bytes 6291460
  7.2 41.0 %copy-start.11 = (bf16[2,128,128]{2,1,0:T(8,128)(2,1)S(1)}, bf16[2,128,128]{2,1,0:T(8,128)(2,1)}, u32[]{:S(2)}) copy-start(bf16[2,128,128]{2,1,0:T(8,128)(2,1)} %param.11) | copy-start | bytes 196612
  7.2 41.0 %copy-start.14 = (bf16[128,8]{0,1:T(8,128)(2,1)S(1)}, bf16[128,8]{0,1:T(8,128)(2,1)}, u32[]{:S(2)}) copy-start(bf16[128,8]{0,1:T(8,128)(2,1)} %param.13) | copy-start | bytes 6148
  7.2 88.4 %all-gather.5.cloned.1.call-start = ((), (), s32[]{:S(2)}) async-start(), calls=%async_computation.20 | async-start | bytes 3244032 | tf_op jit(solution)/shard_map/all_gather | solution.py:83
  32.8 130.4 %all-gather.7.cloned.1.call-start = ((), (), s32[]{:S(2)}) async-start(), calls=%async_computation.21 | async-start | bytes 3244032 | tf_op jit(solution)/shard_map/all_gather | solution.py:83
  95.6 3.7 copy-start.3
  95.6 4.1 copy-start.7
  99.7 1.8 copy-start.15
  114.3 53.2 %all-to-all-start.2 = ((bf16[2,16,128,384]{2,1,3,0:T(8,128)(2,1)}), bf16[2,16,128,384]{2,1,3,0:T(8,128)(2,1)}, u32[]{:S(2)}, u32[]{:S(2)}) async-start(bf16[2,16,128,384]{2,1,3,0:T(8,128)(2,1)} %bitcast.266), calls=%async_computation.2 | async-start | bytes 6291456 | tf_op jit(solution)/shard_map/all_to_all | solution.py:31
  168.2 29.7 %all-to-all-start = ((f32[32,2,128,8]{2,3,1,0:T(8,128)}), f32[32,2,128,8]{2,3,1,0:T(8,128)S(1)}, u32[]{:S(2)}, u32[]{:S(2)}) async-start(f32[32,2,128,8]{2,3,1,0:T(8,128)} %broadcast_in_dim.162), calls=%async_computation | async-start | bytes 524288 | tf_op jit(solution)/shard_map/all_to_all | solution.py:13
  208.3 45.1 %all-to-all-start.3 = ((bf16[16,128,384]{1,2,0:T(8,128)(2,1)}), bf16[16,128,384]{1,2,0:T(8,128)(2,1)}, u32[]{:S(2)}, u32[]{:S(2)}) async-start(bf16[16,128,384]{1,2,0:T(8,128)(2,1)} %copy.78), calls=%async_computation.3 | async-start | bytes 3145728 | tf_op jit(solution)/shard_map/all_to_all | solution.py:39
  220.4 38.5 %copy-start.12 = (bf16[2,128,128]{2,1,0:T(8,128)(2,1)S(1)}, bf16[2,128,128]{2,1,0:T(8,128)(2,1)}, u32[]{:S(2)}) copy-start(bf16[2,128,128]{2,1,0:T(8,128)(2,1)} %param.17) | copy-start | bytes 196612
  220.4 40.0 %copy-start.13 = (s32[2,128,2]{1,2,0:T(2,128)S(1)}, s32[2,128,2]{1,2,0:T(2,128)}, u32[]{:S(2)}) copy-start(s32[2,128,2]{1,2,0:T(2,128)} %param.12) | copy-start | bytes 6148
  253.4 41.4 %all-to-all-start.7 = ((bf16[16,128,384]{1,2,0:T(8,128)(2,1)}), bf16[16,128,384]{1,2,0:T(8,128)(2,1)}, u32[]{:S(2)}, u32[]{:S(2)}) async-start(bf16[16,128,384]{1,2,0:T(8,128)(2,1)} %copy.84), calls=%async_computation.7 | async-start | bytes 3145728 | tf_op jit(solution)/shard_map/all_to_all | solution.py:39
  294.8 18.3 %all-to-all-start.4 = ((bf16[128,8,48]{0,2,1:T(8,128)(2,1)}), bf16[128,8,48]{0,2,1:T(8,128)(2,1)S(1)}, u32[]{:S(2)}, u32[]{:S(2)}) async-start(bf16[128,8,48]{0,2,1:T(8,128)(2,1)} %bitcast.15), calls=%async_computation.4 | async-start | bytes 196608 | tf_op jit(solution)/shard_map/all_to_all | solution.py:88
  313.2 13.7 %all-to-all-start.8 = ((bf16[128,8,48]{0,2,1:T(8,128)(2,1)}), bf16[128,8,48]{0,2,1:T(8,128)(2,1)S(1)}, u32[]{:S(2)}, u32[]{:S(2)}) async-start(bf16[128,8,48]{0,2,1:T(8,128)(2,1)} %bitcast.34), calls=%async_computation.8 | async-start | bytes 196608 | tf_op jit(solution)/shard_map/all_to_all | solution.py:88
  329.1 12.7 %all-to-all-start.18 = ((f32[32,2,128]{2,1,0:T(2,128)}), f32[32,2,128]{2,1,0:T(2,128)S(1)}, u32[]{:S(2)}, u32[]{:S(2)}) async-start(f32[32,2,128]{2,1,0:T(2,128)} %broadcast_in_dim.180), calls=%async_computation.18 | async-start | bytes 65536 | tf_op jit(solution)/shard_map/all_to_all | solution.py:13
  335.3 82.9 %all-gather.11.cloned.1.call-start = ((), (), s32[]{:S(2)}) async-start(), calls=%async_computation.23 | async-start | bytes 3244032 | tf_op jit(solution)/shard_map/all_gather | solution.py:83
  358.5 10.9 %all-to-all-start.13 = ((f32[32,2,128]{2,1,0:T(2,128)}), f32[32,2,128]{2,1,0:T(2,128)S(1)}, u32[]{:S(2)}, u32[]{:S(2)}) async-start(f32[32,2,128]{2,1,0:T(2,128)} %broadcast_in_dim.178), calls=%async_computation.13 | async-start | bytes 65536 | tf_op jit(solution)/shard_map/all_to_all | solution.py:13
  362.8 123.2 %all-gather.9.cloned.1.call-start = ((), (), s32[]{:S(2)}) async-start(), calls=%async_computation.22 | async-start | bytes 3244032 | tf_op jit(solution)/shard_map/all_gather | solution.py:83
  418.1 3.2 copy-start.5
  435.8 57.2 %all-to-all-start.15 = ((bf16[2,16,128,384]{2,1,3,0:T(8,128)(2,1)}), bf16[2,16,128,384]{2,1,3,0:T(8,128)(2,1)}, u32[]{:S(2)}, u32[]{:S(2)}) async-start(bf16[2,16,128,384]{2,1,3,0:T(8,128)(2,1)} %bitcast.265), calls=%async_computation.15 | async-start | bytes 6291456 | tf_op jit(solution)/shard_map/all_to_all | solution.py:31
  486.0 3.3 copy-start.6
  489.3 12.4 %copy-start.9 = (bf16[1,4096,256]{2,1,0:T(8,128)(2,1)S(1)}, bf16[1,4096,256]{2,1,0:T(8,128)(2,1)}, u32[]{:S(2)}) copy-start(bf16[1,4096,256]{2,1,0:T(8,128)(2,1)} %param.15) | copy-start | bytes 6291460
  493.6 28.6 %all-to-all-start.19 = ((f32[8,128,8]{1,2,0:T(8,128)}), f32[8,128,8]{1,2,0:T(8,128)S(1)}, u32[]{:S(2)}, u32[]{:S(2)}) async-start(f32[8,128,8]{1,2,0:T(8,128)} %broadcast_in_dim.184), calls=%async_computation.19 | async-start | bytes 65536 | tf_op jit(solution)/shard_map/all_to_all | solution.py:13
  532.6 42.2 %all-to-all-start.16 = ((bf16[16,128,384]{1,2,0:T(8,128)(2,1)}), bf16[16,128,384]{1,2,0:T(8,128)(2,1)S(1)}, u32[]{:S(2)}, u32[]{:S(2)}) async-start(bf16[16,128,384]{1,2,0:T(8,128)(2,1)} %copy.91), calls=%async_computation.16 | async-start | bytes 3145728 | tf_op jit(solution)/shard_map/all_to_all | solution.py:39
  575.9 41.5 %all-to-all-start.11 = ((bf16[16,128,384]{1,2,0:T(8,128)(2,1)}), bf16[16,128,384]{1,2,0:T(8,128)(2,1)S(1)}, u32[]{:S(2)}, u32[]{:S(2)}) async-start(bf16[16,128,384]{1,2,0:T(8,128)(2,1)} %copy.87), calls=%async_computation.11 | async-start | bytes 3145728 | tf_op jit(solution)/shard_map/all_to_all | solution.py:39
  583.3 3.3 copy-start.4
  586.6 1.9 copy-start.2
  617.4 20.1 %all-to-all-start.17 = ((bf16[128,8,48]{0,2,1:T(8,128)(2,1)}), bf16[128,8,48]{0,2,1:T(8,128)(2,1)S(1)}, u32[]{:S(2)}, u32[]{:S(2)}) async-start(bf16[128,8,48]{0,2,1:T(8,128)(2,1)} %bitcast.65), calls=%async_computation.17 | async-start | bytes 196608 | tf_op jit(solution)/shard_map/all_to_all | solution.py:88
  637.6 15.6 %all-to-all-start.12 = ((bf16[128,8,48]{0,2,1:T(8,128)(2,1)}), bf16[128,8,48]{0,2,1:T(8,128)(2,1)S(1)}, u32[]{:S(2)}, u32[]{:S(2)}) async-start(bf16[128,8,48]{0,2,1:T(8,128)(2,1)} %bitcast.47), calls=%async_computation.12 | async-start | bytes 196608 | tf_op jit(solution)/shard_map/all_to_all | solution.py:88
  642.6 13.2 %copy-start.1 = (bf16[1,256,4096]{2,1,0:T(8,128)(2,1)S(1)}, bf16[1,256,4096]{2,1,0:T(8,128)(2,1)}, u32[]{:S(2)}) copy-start(bf16[1,256,4096]{2,1,0:T(8,128)(2,1)} %param.16) | copy-start | bytes 6291460
  (2 other events, 2.7 us)
Sparse Core Ops, SparseCore 0:
  32.9 62.6 all-gather.4
  97.4 65.8 all-gather.6
  356.5 61.5 all-gather.10
  419.8 66.1 all-gather.8
where the time goes:
time: 673 us; the launch traced here: 662 us
  waiting for transfers between devices  321 us (48%)
  starting transfers between devices  85.1 us (13%)
  blocking collectives  83 us (12%)
  local copies, waits for them, and re-layouts  69.5 us (10%)
  matrix products  60.5 us (9%)
  other arithmetic  28.9 us (4%)
  between operations  14.5 us (2%)
    all_gather x4, waiting for transfers between devices, deliver(): result = lax.all_gather(moved, REP, axis=1, tiled=True)  169 us
    all_to_all x4, waiting for transfers between devices, sum_by_axis(): lax.all_to_all(nearer.astype(jnp.bfloat16), far, split_axis=0, concat_axi...  113 us
    all_to_all x4, blocking collectives, deliver(): lax.all_to_all(pack(rows, source_row, filled, scale), 'ep', split_axis=0,...  62.3 us
    another operation x8, local copies, waits for them, and re-layouts, split_up(): array.reshape(*dims[:dim], devices, dims[dim] // devices, *dims[dim + 1:])  40.2 us
    all_to_all x4, starting transfers between devices, collect(): lax.all_to_all(columns, 'ep', split_axis=1, concat_axis=1, tiled=True)  25.7 us
    all_to_all x4, waiting for transfers between devices, collect(): lax.all_to_all(columns, 'ep', split_axis=1, concat_axis=1, tiled=True)  24.9 us
    all_to_all x4, starting transfers between devices, sum_by_axis(): lax.all_to_all(nearer.astype(jnp.bfloat16), far, split_axis=0, concat_axi...  24.6 us
    all_to_all x4, starting transfers between devices, copy_for_each(): lax.all_to_all(jnp.broadcast_to(array[None], (devices, *array.shape)), ax...  24.1 us
  transfers between devices with their start and end apart: 18, of which 14 were waited for; matrix products, arithmetic and copies ran while one was open for 22% of the time, Pallas kernels for 0%

commit v1 on v0

--- a/solution.py
+++ b/solution.py
@@ -85,7 +85,10 @@
 
 
 def collect(columns):
-    return lax.all_to_all(columns, "ep", split_axis=1, concat_axis=1, tiled=True)
+    return jnp.concatenate(
+        lax.all_to_all(jnp.stack(jnp.split(columns, lax.axis_size("ep"), axis=1)), "ep", 0, 0),
+        axis=1,
+    )
 
 
 def shards(tokens, expert_ids, router_weight, w_gate, w_up, w_down, cotangent):

time: 673 us -> 675 us (level)
  local copies, waits for them, and re-layouts: 69.5 us -> 87.9 us
  waiting for transfers between devices: 321 us -> 304 us
    unnamed x32 -> x62, local copies, waits for them, and re-layouts: 2.77 us -> 18.6 us
    all_to_all x4, waiting for transfers between devices: 113 us -> 101 us  [sum_by_axis(): lax.all_to_all(nearer.astype(jnp.bfloat16), far, split_axis=0, concat_axi...]
  transfers between devices with their start and end apart: 18 -> 18, of which waited for: 14 -> 14; matrix products, arithmetic and copies ran while one was open for 22% -> 24% of each run, Pallas kernels for 0% -> 0%
where the time goes in v1:
time: 675 us; the launch traced here: 664 us
  waiting for transfers between devices  304 us (45%)
  local copies, waits for them, and re-layouts  87.9 us (13%)
  starting transfers between devices  87.3 us (13%)
  blocking collectives  83 us (12%)
  matrix products  60.6 us (9%)
  other arithmetic  26.3 us (4%)
  between operations  14.5 us (2%)
    all_gather x4, waiting for transfers between devices, deliver(): result = lax.all_gather(moved, REP, axis=1, tiled=True)  170 us
    all_to_all x4, waiting for transfers between devices, sum_by_axis(): lax.all_to_all(nearer.astype(jnp.bfloat16), far, split_axis=0, concat_axi...  101 us
    all_to_all x4, blocking collectives, deliver(): lax.all_to_all(pack(rows, source_row, filled, scale), 'ep', split_axis=0,...  62.4 us
    another operation x8, local copies, waits for them, and re-layouts, split_up(): array.reshape(*dims[:dim], devices, dims[dim] // devices, *dims[dim + 1:])  40.3 us
    all_to_all x4, starting transfers between devices, collect(): lax.all_to_all(jnp.stack(jnp.split(columns, lax.axis_size('ep'), axis=1))...  28.3 us
    all_to_all x4, starting transfers between devices, sum_by_axis(): lax.all_to_all(nearer.astype(jnp.bfloat16), far, split_axis=0, concat_axi...  24.7 us
    all_to_all x4, starting transfers between devices, copy_for_each(): lax.all_to_all(jnp.broadcast_to(array[None], (devices, *array.shape)), ax...  23.6 us
    dot_general x6, matrix products, contract_first(): lax.dot_general(left, right, (((0,), (0,)), ((), ())), preferred_element_...  21 us
  transfers between devices with their start and end apart: 18, of which 14 were waited for; matrix products, arithmetic and copies ran while one was open for 24% of the time, Pallas kernels for 0%

profile of v1, /device:TPU:32, one launch (start us, length us, event | category | flops | bytes accessed | tf_op | source)
XLA Modules:
  0.0 663.9 jit_solution(9850137715980807405)
XLA Ops:
  12.3 20.5 %all_to_all.128 = bf16[8,48,128]{2,1,0:T(8,128)(2,1)} all-to-all(bf16[8,48,128]{2,1,0:T(8,128)(2,1)S(1)} %bitcast.415), channel_id=1, replica_groups=mesh['rep_0'=4,'rep_1'=4,'rep_2'=2,'ep'=8] {'ep'}, dimensions={0} | all-to-all | bytes 196608 | tf_op jit(solution)/shard_map/all_to_all | solution.py:80
  34.8 13.4 %all_to_all.129 = bf16[8,48,128]{2,1,0:T(8,128)(2,1)} all-to-all(bf16[8,48,128]{2,1,0:T(8,128)(2,1)S(1)} %bitcast.416), channel_id=1, replica_groups=mesh['rep_0'=4,'rep_1'=4,'rep_2'=2,'ep'=8] {'ep'}, dimensions={0} | all-to-all | bytes 196608 | tf_op jit(solution)/shard_map/all_to_all | solution.py:80
  48.4 47.2 %all-gather.5.cloned.1.call-done = bf16[384,4096]{1,0:T(8,128)(2,1)} async-done(((bf16[384,128]{1,0:T(8,128)(2,1)}), bf16[384,4096]{1,0:T(8,128)(2,1)}) %all-gather.5.cloned.1.call-update) | async-done | bytes 3145744 | tf_op jit(solution)/shard_map/all_gather | solution.py:83
  104.1 6.2 reshape_reshape.12
  119.4 43.9 %all-gather.7.cloned.1.call-done = bf16[384,4096]{1,0:T(8,128)(2,1)} async-done(((bf16[384,128]{1,0:T(8,128)(2,1)}), bf16[384,4096]{1,0:T(8,128)(2,1)}) %all-gather.7.cloned.1.call-update) | async-done | bytes 3145744 | tf_op jit(solution)/shard_map/all_gather | solution.py:83
  168.2 5.6 all-to-all-start
  187.9 6.2 reshape_reshape.13
  198.1 10.3 %all_to_all.130 = bf16[2,16,128,384]{2,1,3,0:T(8,128)(2,1)} all-to-all(bf16[2,16,128,384]{2,1,3,0:T(8,128)(2,1)} %bitcast.399), channel_id=1, replica_groups=mesh['rep_0'=4,'rep_1'=4,'rep_2'=2,'ep'=8] {'rep_2'}, dimensions={0} | all-to-all | bytes 6291456 | tf_op jit(solution)/shard_map/all_to_all | solution.py:31
  208.4 8.0 %all-to-all-start.3 = ((bf16[16,128,384]{1,2,0:T(8,128)(2,1)}), bf16[16,128,384]{1,2,0:T(8,128)(2,1)}, u32[]{:S(2)}, u32[]{:S(2)}) async-start(bf16[16,128,384]{1,2,0:T(8,128)(2,1)} %copy.78), calls=%async_computation.3 | async-start | bytes 3145728 | tf_op jit(solution)/shard_map/all_to_all | solution.py:39
  223.5 30.0 %all-to-all-done.3 = bf16[16,128,384]{1,2,0:T(8,128)(2,1)} async-done(((bf16[16,128,384]{1,2,0:T(8,128)(2,1)}), bf16[16,128,384]{1,2,0:T(8,128)(2,1)}, u32[]{:S(2)}, u32[]{:S(2)}) %all-to-all-start.3) | async-done | bytes 1572896 | tf_op jit(solution)/shard_map/all_to_all | solution.py:39
  253.5 5.5 all-to-all-start.7
  267.1 27.8 %all-to-all-done.7 = bf16[16,128,384]{1,2,0:T(8,128)(2,1)} async-done(((bf16[16,128,384]{1,2,0:T(8,128)(2,1)}), bf16[16,128,384]{1,2,0:T(8,128)(2,1)}, u32[]{:S(2)}, u32[]{:S(2)}) %all-to-all-start.7) | async-done | bytes 1572896 | tf_op jit(solution)/shard_map/all_to_all | solution.py:39
  294.9 7.8 %all-to-all-start.4 = ((bf16[8,128,48]{1,2,0:T(8,128)(2,1)}), bf16[8,128,48]{1,2,0:T(8,128)(2,1)S(1)}, u32[]{:S(2)}, u32[]{:S(2)}) async-start(bf16[8,128,48]{1,2,0:T(8,128)(2,1)} %constant_dynamic-update-slice_fusion), calls=%async_computation.4 | async-start | bytes 196608 | tf_op jit(solution)/shard_map/all_to_all | solution.py:89
  313.3 5.5 all-to-all-start.8
  320.2 9.1 %all-to-all-done.8 = bf16[8,128,48]{1,2,0:T(8,128)(2,1)S(1)} async-done(((bf16[8,128,48]{1,2,0:T(8,128)(2,1)}), bf16[8,128,48]{1,2,0:T(8,128)(2,1)S(1)}, u32[]{:S(2)}, u32[]{:S(2)}) %all-to-all-start.8) | async-done | bytes 98336 | tf_op jit(solution)/shard_map/all_to_all | solution.py:89
  331.6 5.6 all-to-all-start.18
  337.3 6.5 all-to-all-done.18
  344.3 14.1 %all_to_all.131 = bf16[8,48,128]{2,1,0:T(8,128)(2,1)} all-to-all(bf16[8,48,128]{2,1,0:T(8,128)(2,1)S(1)} %bitcast.413), channel_id=1, replica_groups=mesh['rep_0'=4,'rep_1'=4,'rep_2'=2,'ep'=8] {'ep'}, dimensions={0} | all-to-all | bytes 196608 | tf_op jit(solution)/shard_map/all_to_all | solution.py:80
  364.9 6.6 all-to-all-done.13
  371.9 14.4 %all_to_all.132 = bf16[8,48,128]{2,1,0:T(8,128)(2,1)} all-to-all(bf16[8,48,128]{2,1,0:T(8,128)(2,1)S(1)} %bitcast.414), channel_id=1, replica_groups=mesh['rep_0'=4,'rep_1'=4,'rep_2'=2,'ep'=8] {'ep'}, dimensions={0} | all-to-all | bytes 196608 | tf_op jit(solution)/shard_map/all_to_all | solution.py:80
  386.5 33.7 %all-gather.11.cloned.1.call-done = bf16[384,4096]{1,0:T(8,128)(2,1)} async-done(((bf16[384,128]{1,0:T(8,128)(2,1)}), bf16[384,4096]{1,0:T(8,128)(2,1)}) %all-gather.11.cloned.1.call-update) | async-done | bytes 3145744 | tf_op jit(solution)/shard_map/all_gather | solution.py:83
  427.8 6.1 reshape_reshape.15
  443.2 44.9 %all-gather.9.cloned.1.call-done = bf16[384,4096]{1,0:T(8,128)(2,1)} async-done(((bf16[384,128]{1,0:T(8,128)(2,1)}), bf16[384,4096]{1,0:T(8,128)(2,1)}) %all-gather.9.cloned.1.call-update) | async-done | bytes 3145744 | tf_op jit(solution)/shard_map/all_gather | solution.py:83
  495.6 8.1 %all-to-all-start.19 = ((f32[8,128,8]{1,2,0:T(8,128)}), f32[8,128,8]{1,2,0:T(8,128)S(1)}, u32[]{:S(2)}, u32[]{:S(2)}) async-start(f32[8,128,8]{1,2,0:T(8,128)} %broadcast_in_dim.184), calls=%async_computation.19 | async-start | bytes 65536 | tf_op jit(solution)/shard_map/all_to_all | solution.py:13
  514.2 6.1 reshape_reshape.14
  524.3 10.4 %all_to_all.133 = bf16[2,16,128,384]{2,1,3,0:T(8,128)(2,1)} all-to-all(bf16[2,16,128,384]{2,1,3,0:T(8,128)(2,1)} %bitcast.400), channel_id=1, replica_groups=mesh['rep_0'=4,'rep_1'=4,'rep_2'=2,'ep'=8] {'rep_2'}, dimensions={0} | all-to-all | bytes 6291456 | tf_op jit(solution)/shard_map/all_to_all | solution.py:31
  555.2 21.7 %all-to-all-done.16 = bf16[16,128,384]{1,2,0:T(8,128)(2,1)S(1)} async-done(((bf16[16,128,384]{1,2,0:T(8,128)(2,1)}), bf16[16,128,384]{1,2,0:T(8,128)(2,1)S(1)}, u32[]{:S(2)}, u32[]{:S(2)}) %all-to-all-start.16) | async-done | bytes 1572896 | tf_op jit(solution)/shard_map/all_to_all | solution.py:39
  576.8 5.9 all-to-all-start.11
  597.1 21.4 %all-to-all-done.11 = bf16[16,128,384]{1,2,0:T(8,128)(2,1)} async-done(((bf16[16,128,384]{1,2,0:T(8,128)(2,1)}), bf16[16,128,384]{1,2,0:T(8,128)(2,1)}, u32[]{:S(2)}, u32[]{:S(2)}) %all-to-all-start.11) | async-done | bytes 1572896 | tf_op jit(solution)/shard_map/all_to_all | solution.py:39
  618.4 9.6 %all-to-all-start.17 = ((bf16[8,128,48]{1,2,0:T(8,128)(2,1)}), bf16[8,128,48]{1,2,0:T(8,128)(2,1)S(1)}, u32[]{:S(2)}, u32[]{:S(2)}) async-start(bf16[8,128,48]{1,2,0:T(8,128)(2,1)} %constant_dynamic-update-slice_fusion.24), calls=%async_computation.17 | async-start | bytes 196608 | tf_op jit(solution)/shard_map/all_to_all | solution.py:89
  638.6 5.5 all-to-all-start.12
  644.0 5.9 fusion.7
  (196 shorter events, 176.3 us)
Async XLA Ops:
  7.2 94.3 %copy-start = (bf16[1,256,4096]{2,1,0:T(8,128)(2,1)S(1)}, bf16[1,256,4096]{2,1,0:T(8,128)(2,1)}, u32[]{:S(2)}) copy-start(bf16[1,256,4096]{2,1,0:T(8,128)(2,1)} %param.16) | copy-start | bytes 6291460
  7.2 41.0 %copy-start.12 = (bf16[2,128,128]{2,1,0:T(8,128)(2,1)S(1)}, bf16[2,128,128]{2,1,0:T(8,128)(2,1)}, u32[]{:S(2)}) copy-start(bf16[2,128,128]{2,1,0:T(8,128)(2,1)} %param.11) | copy-start | bytes 196612
  7.2 41.0 %copy-start.15 = (bf16[128,8]{0,1:T(8,128)(2,1)S(1)}, bf16[128,8]{0,1:T(8,128)(2,1)}, u32[]{:S(2)}) copy-start(bf16[128,8]{0,1:T(8,128)(2,1)} %param.13) | copy-start | bytes 6148
  7.2 88.4 %all-gather.5.cloned.1.call-start = ((), (), s32[]{:S(2)}) async-start(), calls=%async_computation.20 | async-start | bytes 3244032 | tf_op jit(solution)/shard_map/all_gather | solution.py:83
  32.8 130.5 %all-gather.7.cloned.1.call-start = ((), (), s32[]{:S(2)}) async-start(), calls=%async_computation.21 | async-start | bytes 3244032 | tf_op jit(solution)/shard_map/all_gather | solution.py:83
  95.6 3.7 copy-start.4
  95.6 4.1 copy-start.8
  114.1 53.4 %all-to-all-start.2 = ((bf16[2,16,128,384]{2,1,3,0:T(8,128)(2,1)}), bf16[2,16,128,384]{2,1,3,0:T(8,128)(2,1)}, u32[]{:S(2)}, u32[]{:S(2)}) async-start(bf16[2,16,128,384]{2,1,3,0:T(8,128)(2,1)} %bitcast.398), calls=%async_computation.2 | async-start | bytes 6291456 | tf_op jit(solution)/shard_map/all_to_all | solution.py:31
  168.2 29.8 %all-to-all-start = ((f32[32,2,128,8]{2,3,1,0:T(8,128)}), f32[32,2,128,8]{2,3,1,0:T(8,128)S(1)}, u32[]{:S(2)}, u32[]{:S(2)}) async-start(f32[32,2,128,8]{2,3,1,0:T(8,128)} %broadcast_in_dim.162), calls=%async_computation | async-start | bytes 524288 | tf_op jit(solution)/shard_map/all_to_all | solution.py:13
  208.4 45.1 %all-to-all-start.3 = ((bf16[16,128,384]{1,2,0:T(8,128)(2,1)}), bf16[16,128,384]{1,2,0:T(8,128)(2,1)}, u32[]{:S(2)}, u32[]{:S(2)}) async-start(bf16[16,128,384]{1,2,0:T(8,128)(2,1)} %copy.78), calls=%async_computation.3 | async-start | bytes 3145728 | tf_op jit(solution)/shard_map/all_to_all | solution.py:39
  220.5 38.5 %copy-start.13 = (bf16[2,128,128]{2,1,0:T(8,128)(2,1)S(1)}, bf16[2,128,128]{2,1,0:T(8,128)(2,1)}, u32[]{:S(2)}) copy-start(bf16[2,128,128]{2,1,0:T(8,128)(2,1)} %param.17) | copy-start | bytes 196612
  220.5 40.0 %copy-start.14 = (s32[2,128,2]{1,2,0:T(2,128)S(1)}, s32[2,128,2]{1,2,0:T(2,128)}, u32[]{:S(2)}) copy-start(s32[2,128,2]{1,2,0:T(2,128)} %param.12) | copy-start | bytes 6148
  253.5 41.4 %all-to-all-start.7 = ((bf16[16,128,384]{1,2,0:T(8,128)(2,1)}), bf16[16,128,384]{1,2,0:T(8,128)(2,1)}, u32[]{:S(2)}, u32[]{:S(2)}) async-start(bf16[16,128,384]{1,2,0:T(8,128)(2,1)} %copy.84), calls=%async_computation.7 | async-start | bytes 3145728 | tf_op jit(solution)/shard_map/all_to_all | solution.py:39
  294.9 18.3 %all-to-all-start.4 = ((bf16[8,128,48]{1,2,0:T(8,128)(2,1)}), bf16[8,128,48]{1,2,0:T(8,128)(2,1)S(1)}, u32[]{:S(2)}, u32[]{:S(2)}) async-start(bf16[8,128,48]{1,2,0:T(8,128)(2,1)} %constant_dynamic-update-slice_fusion), calls=%async_computation.4 | async-start | bytes 196608 | tf_op jit(solution)/shard_map/all_to_all | solution.py:89
  313.3 16.1 %all-to-all-start.8 = ((bf16[8,128,48]{1,2,0:T(8,128)(2,1)}), bf16[8,128,48]{1,2,0:T(8,128)(2,1)S(1)}, u32[]{:S(2)}, u32[]{:S(2)}) async-start(bf16[8,128,48]{1,2,0:T(8,128)(2,1)} %constant_dynamic-update-slice_fusion.8), calls=%async_computation.8 | async-start | bytes 196608 | tf_op jit(solution)/shard_map/all_to_all | solution.py:89
  331.6 12.2 %all-to-all-start.18 = ((f32[32,2,128]{2,1,0:T(2,128)}), f32[32,2,128]{2,1,0:T(2,128)S(1)}, u32[]{:S(2)}, u32[]{:S(2)}) async-start(f32[32,2,128]{2,1,0:T(2,128)} %broadcast_in_dim.180), calls=%async_computation.18 | async-start | bytes 65536 | tf_op jit(solution)/shard_map/all_to_all | solution.py:13
  337.3 82.9 %all-gather.11.cloned.1.call-start = ((), (), s32[]{:S(2)}) async-start(), calls=%async_computation.23 | async-start | bytes 3244032 | tf_op jit(solution)/shard_map/all_gather | solution.py:83
  360.5 10.9 %all-to-all-start.13 = ((f32[32,2,128]{2,1,0:T(2,128)}), f32[32,2,128]{2,1,0:T(2,128)S(1)}, u32[]{:S(2)}, u32[]{:S(2)}) async-start(f32[32,2,128]{2,1,0:T(2,128)} %broadcast_in_dim.178), calls=%async_computation.13 | async-start | bytes 65536 | tf_op jit(solution)/shard_map/all_to_all | solution.py:13
  364.8 123.2 %all-gather.9.cloned.1.call-start = ((), (), s32[]{:S(2)}) async-start(), calls=%async_computation.22 | async-start | bytes 3244032 | tf_op jit(solution)/shard_map/all_gather | solution.py:83
  420.2 3.3 copy-start.6
  437.8 57.2 %all-to-all-start.15 = ((bf16[2,16,128,384]{2,1,3,0:T(8,128)(2,1)}), bf16[2,16,128,384]{2,1,3,0:T(8,128)(2,1)}, u32[]{:S(2)}, u32[]{:S(2)}) async-start(bf16[2,16,128,384]{2,1,3,0:T(8,128)(2,1)} %bitcast.397), calls=%async_computation.15 | async-start | bytes 6291456 | tf_op jit(solution)/shard_map/all_to_all | solution.py:31
  488.0 3.2 copy-start.7
  491.3 12.4 %copy-start.10 = (bf16[1,4096,256]{2,1,0:T(8,128)(2,1)S(1)}, bf16[1,4096,256]{2,1,0:T(8,128)(2,1)}, u32[]{:S(2)}) copy-start(bf16[1,4096,256]{2,1,0:T(8,128)(2,1)} %param.15) | copy-start | bytes 6291460
  495.6 28.7 %all-to-all-start.19 = ((f32[8,128,8]{1,2,0:T(8,128)}), f32[8,128,8]{1,2,0:T(8,128)S(1)}, u32[]{:S(2)}, u32[]{:S(2)}) async-start(f32[8,128,8]{1,2,0:T(8,128)} %broadcast_in_dim.184), calls=%async_computation.19 | async-start | bytes 65536 | tf_op jit(solution)/shard_map/all_to_all | solution.py:13
  534.6 42.2 %all-to-all-start.16 = ((bf16[16,128,384]{1,2,0:T(8,128)(2,1)}), bf16[16,128,384]{1,2,0:T(8,128)(2,1)S(1)}, u32[]{:S(2)}, u32[]{:S(2)}) async-start(bf16[16,128,384]{1,2,0:T(8,128)(2,1)} %copy.91), calls=%async_computation.16 | async-start | bytes 3145728 | tf_op jit(solution)/shard_map/all_to_all | solution.py:39
  548.6 3.4 copy-start.5
  576.8 41.6 %all-to-all-start.11 = ((bf16[16,128,384]{1,2,0:T(8,128)(2,1)}), bf16[16,128,384]{1,2,0:T(8,128)(2,1)}, u32[]{:S(2)}, u32[]{:S(2)}) async-start(bf16[16,128,384]{1,2,0:T(8,128)(2,1)} %copy.87), calls=%async_computation.11 | async-start | bytes 3145728 | tf_op jit(solution)/shard_map/all_to_all | solution.py:39
  582.7 3.4 copy-start.2
  582.7 4.1 copy-start.3
  618.4 20.1 %all-to-all-start.17 = ((bf16[8,128,48]{1,2,0:T(8,128)(2,1)}), bf16[8,128,48]{1,2,0:T(8,128)(2,1)S(1)}, u32[]{:S(2)}, u32[]{:S(2)}) async-start(bf16[8,128,48]{1,2,0:T(8,128)(2,1)} %constant_dynamic-update-slice_fusion.24), calls=%async_computation.17 | async-start | bytes 196608 | tf_op jit(solution)/shard_map/all_to_all | solution.py:89
  638.6 16.0 %all-to-all-start.12 = ((bf16[8,128,48]{1,2,0:T(8,128)(2,1)}), bf16[8,128,48]{1,2,0:T(8,128)(2,1)S(1)}, u32[]{:S(2)}, u32[]{:S(2)}) async-start(bf16[8,128,48]{1,2,0:T(8,128)(2,1)} %constant_dynamic-update-slice_fusion.16), calls=%async_computation.12 | async-start | bytes 196608 | tf_op jit(solution)/shard_map/all_to_all | solution.py:89
  644.0 13.2 %copy-start.1 = (bf16[1,256,4096]{2,1,0:T(8,128)(2,1)S(1)}, bf16[1,256,4096]{2,1,0:T(8,128)(2,1)}, u32[]{:S(2)}) copy-start(bf16[1,256,4096]{2,1,0:T(8,128)(2,1)} %param.16) | copy-start | bytes 6291460
  (3 other events, 6.4 us)
Sparse Core Ops, SparseCore 0:
  32.9 62.6 all-gather.4
  97.4 65.8 all-gather.6
  358.5 61.5 all-gather.10
  421.8 66.1 all-gather.8
